TPU v7x, 256 devices: a whole 4x4x8 slice. The times are simulated.
256 devices in a mesh: grp: 4 (over y), dev: 64 (over x, z, core).
Axes of the slice: x: 4, y: 4, z: 8, core: 2. Of those that a mesh axis runs over, the one named last changes fastest.
Arguments:
- pool_rows: bfloat16 [262144, 1024], P(('grp', 'dev')), may hold values from -6 to 6
- sample_index: int32 [262144], P(('grp', 'dev')), may hold values from 0 to 262143, as said below
- cluster_id: int32 [262144], P(('grp', 'dev')), may hold values from 0 to 511, as said below
- child_id: int32 [262144], P(('grp', 'dev')), may hold values from 0 to 7
- old_centroids: float32 [512, 8, 1024], P('dev'), may hold values from -6 to 6
Outputs:
- centroids: float32 [512, 8, 1024], P('dev')
- child_counts: int32 [512, 8], P('dev')
Inputs may be any that keep to these rules, and one draw needn't show every extreme that they name: Sample i takes a pool row of its own aligned block of 1024 rows: sample_index[i] // 1024 == i // 1024. `cluster_id`: in each aligned block of 1024 samples (the rows of one device) the 2 clusters o * 2 to o * 2 + 1 of any owner o are named at most 8 times together, and one cluster, the same in every block, is named exactly 8 times in every block.
All inputs are finite; a program needn't handle non-finite values.
Results may differ from a plain program's by a relative error of at most 0.0003.
Values may be sent and summed in bfloat16 or wider, within the bound.
A program may use at most 64 MiB of HBM per device.

v0:
```python
import math
import jax
import jax.numpy as jnp
from jax import lax
from jax.sharding import PartitionSpec as P


def side_by_side(arrays, axis, dim, along):
    widths = [math.prod(a.shape[along:]) for a in arrays]
    both = jnp.concatenate(
        [a.reshape(*a.shape[:along], w) for a, w in zip(arrays, widths)], axis=along
    )
    filled = lax.all_gather(both, axis, axis=dim, tiled=True)
    parts = jnp.split(filled, [sum(widths[:k]) for k in range(1, len(widths))], axis=along)
    return tuple(
        (b.reshape(*filled.shape[:along], *a.shape[along:]) for a, b in zip(arrays, parts))
    )


def segment_totals(rows, segment, segments):
    onehot = (jnp.arange(segments, dtype=jnp.int32)[:, None] == segment[None, :]).astype(
        jnp.bfloat16
    )
    sums = jnp.dot(onehot, rows, preferred_element_type=jnp.float32)
    counts = jnp.sum(onehot.astype(jnp.float32), axis=1)
    return (sums, counts)


def rank_within(keys_here):
    positions = jnp.arange(keys_here.shape[0], dtype=jnp.int32)
    matches = keys_here[:, None] == keys_here[None, :]
    earlier = positions[None, :] < positions[:, None]
    return jnp.sum(matches & earlier, axis=1)


def per_device(pool_rows, sample_index, cluster_id, child_id, old_centroids):
    rows_dev, row_width = pool_rows.shape
    block_clusters, kinds = (old_centroids.shape[0], old_centroids.shape[1])
    groups = lax.axis_size("grp")
    owners = lax.axis_size("dev")
    owned = block_clusters // groups
    clusters = block_clusters * owners
    most = 4 * rows_dev // clusters
    sample = pool_rows[sample_index % rows_dev]
    holder_table = cluster_id // owned
    slot_of = holder_table * most + rank_within(holder_table)
    total_slots = clusters // owned * most
    label_of = cluster_id % owned * kinds + child_id
    buffer = jnp.zeros((total_slots, row_width), jnp.bfloat16).at[slot_of].set(sample)
    labels = jnp.full((total_slots,), -1, jnp.int32).at[slot_of].set(label_of)
    shaped = buffer.reshape(owners, groups, most, row_width)
    shaped_labels = labels.reshape(owners, groups, most)
    arrived, arrived_labels = (
        lax.all_to_all(
            lax.all_to_all(shaped, "dev", split_axis=0, concat_axis=0, tiled=True),
            "grp",
            split_axis=1,
            concat_axis=1,
            tiled=True,
        ),
        lax.all_to_all(
            lax.all_to_all(shaped_labels, "dev", split_axis=0, concat_axis=0, tiled=True),
            "grp",
            split_axis=1,
            concat_axis=1,
            tiled=True,
        ),
    )
    sums, counts = segment_totals(
        arrived.reshape(-1, row_width), arrived_labels.reshape(-1), owned * kinds
    )
    group_index = lax.axis_index("grp")
    mine = lax.dynamic_slice_in_dim(old_centroids, group_index * owned, owned, 0)
    counts_owned = counts.reshape(owned, kinds)
    fresh = (sums.reshape(owned, kinds, row_width) + mine) / (counts_owned[:, :, None] + 1.0)
    centroids, new_counts = side_by_side((fresh, counts_owned), "grp", 0, 2)
    return (centroids, new_counts.astype(jnp.int32))


def solution(mesh):
    placed = (
        P(("grp", "dev"), None),
        P(("grp", "dev")),
        P(("grp", "dev")),
        P(("grp", "dev")),
        P("dev", None, None),
    )
    return jax.shard_map(
        per_device,
        mesh=mesh,
        in_specs=placed,
        out_specs=(P("dev", None, None), P("dev", None)),
        check_vma=False,
    )
```

profile of v0, /device:TPU:2, one launch (start us, length us, event | category | flops | bytes accessed | tf_op | source)
XLA Modules:
  0.0 222.8 jit_solution(11543515831146436987)
XLA Ops:
  0.6 0.0 copy-start
  0.6 0.8 add_select_fusion.2
  1.5 0.5 convert_reduce_fusion
  2.0 0.7 fusion.10
  2.8 4.3 %scatter_custom_fusion = s32[2048]{0:T(1024)S(1)} fusion(s32[1024]{0:T(1024)S(1)} %get-tuple-element.3, s32[1024]{0:T(1024)S(1)} %get-tuple-element.2, s32[]{:T(128)} %constant.47.clone.1), kind=kCustom, calls=%fused_computation.34 | custom fusion | bytes 8196 | tf_op jit(solution)/shard_map/scatter | solution.py:50
  7.1 0.8 reshape.46
  7.9 12.0 %all-to-all-start = ((s32[64,4,8]{2,1,0:T(4,128)}), s32[64,4,8]{2,1,0:T(4,128)S(1)}, u32[]{:S(2)}, u32[]{:S(2)}) async-start(s32[64,4,8]{2,1,0:T(4,128)} %reshape.46), calls=%async_computation | async-start | bytes 262144 | tf_op jit(solution)/shard_map/all_to_all | solution.py:62
  20.0 0.0 copy-done
  20.0 15.3 %scatter_custom_fusion.1 = bf16[2048,1024]{1,0:T(8,128)(2,1)} fusion(s32[1024]{0:T(1024)S(1)} %get-tuple-element.3, bf16[1024,1024]{1,0:T(8,128)(2,1)S(1)} %copy-done, s32[1024]{0:T(1024)S(1)} %get-tuple-element.4, bf16[]{:T(256)} %constant.52.clone.1), kind=kCustom, calls=%fused_computation.6 | custom fusion | bytes 4194306 | tf_op jit(solution)/shard_map/scatter | solution.py:49
  35.3 0.0 all-to-all-done
  35.3 10.5 %all-to-all-start.2 = ((bf16[64,4,8,1024]{3,2,1,0:T(8,128)(2,1)}), bf16[64,4,8,1024]{3,2,1,0:T(8,128)(2,1)}, u32[]{:S(2)}, u32[]{:S(2)}) async-start(bf16[64,4,8,1024]{3,2,1,0:T(8,128)(2,1)} %bitcast.10), calls=%async_computation.2 | async-start | bytes 8388608 | tf_op jit(solution)/shard_map/all_to_all | solution.py:55
  45.8 0.1 copy.20
  45.9 0.7 reshape.85
  46.6 94.0 %all-to-all-done.2 = bf16[64,4,8,1024]{3,2,1,0:T(8,128)(2,1)} async-done(((bf16[64,4,8,1024]{3,2,1,0:T(8,128)(2,1)}), bf16[64,4,8,1024]{3,2,1,0:T(8,128)(2,1)}, u32[]{:S(2)}, u32[]{:S(2)}) %all-to-all-start.2) | async-done | bytes 4194336 | tf_op jit(solution)/shard_map/all_to_all | solution.py:55
  140.5 4.5 %all-to-all-start.1 = ((s32[4,1,512]{2,1,0:T(1,128)}), s32[4,1,512]{2,1,0:T(1,128)S(1)}, u32[]{:S(2)}, u32[]{:S(2)}) async-start(s32[4,1,512]{2,1,0:T(1,128)} %reshape.85), calls=%async_computation.1 | async-start | bytes 16384 | tf_op jit(solution)/shard_map/all_to_all | solution.py:61
  145.0 4.8 %copy.22 = bf16[64,4,8,1024]{3,2,0,1:T(8,128)(2,1)} copy(bf16[64,4,8,1024]{3,2,1,0:T(8,128)(2,1)} %all-to-all-done.2) | data formatting | bytes 8388608 | tf_op jit(solution)/shard_map/all_to_all | solution.py:55
  149.8 0.6 all-to-all-done.1
  150.3 4.9 %all-to-all-start.3 = ((bf16[64,4,8,1024]{3,2,0,1:T(8,128)(2,1)}), bf16[64,4,8,1024]{3,2,0,1:T(8,128)(2,1)}, u32[]{:S(2)}, u32[]{:S(2)}) async-start(bf16[64,4,8,1024]{3,2,0,1:T(8,128)(2,1)} %copy.22), calls=%async_computation.3 | async-start | bytes 8388608 | tf_op jit(solution)/shard_map/all_to_all | solution.py:54
  155.2 0.5 broadcast.69
  155.7 0.7 reduce
  156.4 0.1 reshape.86
  156.5 0.1 copy.21
  156.6 0.2 eq.55
  156.7 0.1 convert_reduce_fusion.1
  156.9 0.1 broadcast_in_dim_reshape.5
  157.0 0.1 add.55
  157.1 47.7 %all-to-all-done.3 = bf16[64,4,8,1024]{3,2,0,1:T(8,128)(2,1)} async-done(((bf16[64,4,8,1024]{3,2,0,1:T(8,128)(2,1)}), bf16[64,4,8,1024]{3,2,0,1:T(8,128)(2,1)}, u32[]{:S(2)}, u32[]{:S(2)}) %all-to-all-start.3) | async-done | bytes 4194336 | tf_op jit(solution)/shard_map/all_to_all | solution.py:54
  204.7 2.6 %copy.23 = bf16[64,4,8,1024]{3,2,1,0:T(8,128)(2,1)S(1)} copy(bf16[64,4,8,1024]{3,2,0,1:T(8,128)(2,1)} %all-to-all-done.3) | data formatting | bytes 8388608 | tf_op jit(solution)/shard_map/all_to_all | solution.py:54
  207.4 1.5 fusion.4
  208.9 12.4 %all_gather.3 = f32[8,8,1025]{2,1,0:T(8,128)S(1)} all-gather(f32[2,8,1025]{2,1,0:T(8,128)S(1)} %pad_maximum_fusion), channel_id=1, replica_groups=mesh['grp'=4,'dev'=64] {'grp'}, dimensions={0}, use_global_device_ids=true | all-gather | bytes 328000 | tf_op jit(solution)/shard_map/all_gather | solution.py:13
  221.4 0.7 split.8
  222.1 0.1 copy.26
  222.2 0.6 convert_bitcast_fusion
  (4 shorter events, 0.0 us)
Async XLA Ops:
  0.6 19.3 %copy-start = (bf16[1024,1024]{1,0:T(8,128)(2,1)S(1)}, bf16[1024,1024]{1,0:T(8,128)(2,1)}, u32[]{:S(2)}) copy-start(bf16[1024,1024]{1,0:T(8,128)(2,1)} %param.5) | copy-start | bytes 6291460
  7.9 27.4 %all-to-all-start = ((s32[64,4,8]{2,1,0:T(4,128)}), s32[64,4,8]{2,1,0:T(4,128)S(1)}, u32[]{:S(2)}, u32[]{:S(2)}) async-start(s32[64,4,8]{2,1,0:T(4,128)} %reshape.46), calls=%async_computation | async-start | bytes 262144 | tf_op jit(solution)/shard_map/all_to_all | solution.py:62
  35.3 105.3 %all-to-all-start.2 = ((bf16[64,4,8,1024]{3,2,1,0:T(8,128)(2,1)}), bf16[64,4,8,1024]{3,2,1,0:T(8,128)(2,1)}, u32[]{:S(2)}, u32[]{:S(2)}) async-start(bf16[64,4,8,1024]{3,2,1,0:T(8,128)(2,1)} %bitcast.10), calls=%async_computation.2 | async-start | bytes 8388608 | tf_op jit(solution)/shard_map/all_to_all | solution.py:55
  140.5 9.8 %all-to-all-start.1 = ((s32[4,1,512]{2,1,0:T(1,128)}), s32[4,1,512]{2,1,0:T(1,128)S(1)}, u32[]{:S(2)}, u32[]{:S(2)}) async-start(s32[4,1,512]{2,1,0:T(1,128)} %reshape.85), calls=%async_computation.1 | async-start | bytes 16384 | tf_op jit(solution)/shard_map/all_to_all | solution.py:61
  150.3 54.4 %all-to-all-start.3 = ((bf16[64,4,8,1024]{3,2,0,1:T(8,128)(2,1)}), bf16[64,4,8,1024]{3,2,0,1:T(8,128)(2,1)}, u32[]{:S(2)}, u32[]{:S(2)}) async-start(bf16[64,4,8,1024]{3,2,0,1:T(8,128)(2,1)} %copy.22), calls=%async_computation.3 | async-start | bytes 8388608 | tf_op jit(solution)/shard_map/all_to_all | solution.py:54
where the time goes:
time: 223 us
  waiting for transfers between devices  142 us (64%)
  starting transfers between devices  31.9 us (14%)
  local copies, waits for them, and re-layouts  30.5 us (14%)
  blocking collectives  12.4 us (6%)
  other arithmetic  3.54 us (2%)
    all_to_all x1, waiting for transfers between devices, per_device(): lax.all_to_all(shaped, 'dev', split_axis=0, concat_axis=0, tiled=True)  94 us
    all_to_all x1, waiting for transfers between devices, per_device(): lax.all_to_all(lax.all_to_all(shaped, 'dev', split_axis=0, concat_axis=0,...  47.7 us
    scatter x1, local copies, waits for them, and re-layouts, per_device(): jnp.zeros((total_slots, row_width), jnp.bfloat16).at[slot_of].set(sample)  15.3 us
    all_gather x1, blocking collectives, side_by_side(): filled = lax.all_gather(both, axis, axis=dim, tiled=True)  12.4 us
    all_to_all x1, starting transfers between devices, per_device(): lax.all_to_all(shaped_labels, 'dev', split_axis=0, concat_axis=0, tiled=T...  12 us
    all_to_all x1, starting transfers between devices, per_device(): lax.all_to_all(shaped, 'dev', split_axis=0, concat_axis=0, tiled=True)  10.5 us
    all_to_all x1, starting transfers between devices, per_device(): lax.all_to_all(lax.all_to_all(shaped, 'dev', split_axis=0, concat_axis=0,...  4.86 us
    all_to_all x1, local copies, waits for them, and re-layouts, per_device(): lax.all_to_all(shaped, 'dev', split_axis=0, concat_axis=0, tiled=True)  4.75 us
  transfers between devices with their start and end apart: 4, of which 3 were waited for; matrix products, arithmetic and copies ran while one was open for 10% of the time, Pallas kernels for 0%

commit v1 on v0

--- a/solution.py
+++ b/solution.py
@@ -3,6 +3,13 @@
 import jax.numpy as jnp
 from jax import lax
 from jax.sharding import PartitionSpec as P
+
+
+def stacked_exchange(shard, name, split, join):
+    size = lax.axis_size(name)
+    blocks = jnp.stack(jnp.split(shard, size, axis=split), axis=0)
+    blocks = lax.all_to_all(blocks, name, split_axis=0, concat_axis=0)
+    return jnp.concatenate(blocks, axis=join)
 
 
 def side_by_side(arrays, axis, dim, along):
@@ -58,12 +65,11 @@
             concat_axis=1,
             tiled=True,
         ),
-        lax.all_to_all(
+        stacked_exchange(
             lax.all_to_all(shaped_labels, "dev", split_axis=0, concat_axis=0, tiled=True),
             "grp",
-            split_axis=1,
-            concat_axis=1,
-            tiled=True,
+            1,
+            1,
         ),
     )
     sums, counts = segment_totals(

time: 223 us -> 223 us (level)
  no operation moved by 1% of the time
where the time goes in v1:
time: 223 us
  waiting for transfers between devices  142 us (64%)
  starting transfers between devices  31.9 us (14%)
  local copies, waits for them, and re-layouts  30.8 us (14%)
  blocking collectives  12.4 us (6%)
  other arithmetic  3.54 us (2%)
    all_to_all x1, waiting for transfers between devices, per_device(): lax.all_to_all(shaped, 'dev', split_axis=0, concat_axis=0, tiled=True)  93.7 us
    all_to_all x1, waiting for transfers between devices, per_device(): lax.all_to_all(lax.all_to_all(shaped, 'dev', split_axis=0, concat_axis=0,...  47.7 us
    scatter x1, local copies, waits for them, and re-layouts, per_device(): jnp.zeros((total_slots, row_width), jnp.bfloat16).at[slot_of].set(sample)  15.3 us
    all_gather x1, blocking collectives, side_by_side(): filled = lax.all_gather(both, axis, axis=dim, tiled=True)  12.4 us
    all_to_all x1, starting transfers between devices, per_device(): lax.all_to_all(shaped_labels, 'dev', split_axis=0, concat_axis=0, tiled=T...  12 us
    all_to_all x1, starting transfers between devices, per_device(): lax.all_to_all(shaped, 'dev', split_axis=0, concat_axis=0, tiled=True)  10.5 us
    all_to_all x1, starting transfers between devices, per_device(): lax.all_to_all(lax.all_to_all(shaped, 'dev', split_axis=0, concat_axis=0,...  4.86 us
    all_to_all x1, local copies, waits for them, and re-layouts, per_device(): lax.all_to_all(shaped, 'dev', split_axis=0, concat_axis=0, tiled=True)  4.75 us
  transfers between devices with their start and end apart: 4, of which 3 were waited for; matrix products, arithmetic and copies ran while one was open for 10% of the time, Pallas kernels for 0%

profile of v1, /device:TPU:2, one launch (start us, length us, event | category | flops | bytes accessed | tf_op | source)
XLA Modules:
  0.0 222.8 jit_solution(9948262098542759407)
XLA Ops:
  0.6 0.0 copy-start
  0.6 0.8 add_select_fusion.2
  1.5 0.5 convert_reduce_fusion
  2.0 0.7 fusion.10
  2.8 4.3 %scatter_custom_fusion = s32[2048]{0:T(1024)S(1)} fusion(s32[1024]{0:T(1024)S(1)} %get-tuple-element.7, s32[1024]{0:T(1024)S(1)} %get-tuple-element.6, s32[]{:T(128)} %constant.47.clone.1), kind=kCustom, calls=%fused_computation.35 | custom fusion | bytes 8196 | tf_op jit(solution)/shard_map/scatter | solution.py:57
  7.1 0.8 reshape.49
  7.9 12.0 %all-to-all-start = ((s32[64,4,8]{2,1,0:T(4,128)}), s32[64,4,8]{2,1,0:T(4,128)S(1)}, u32[]{:S(2)}, u32[]{:S(2)}) async-start(s32[64,4,8]{2,1,0:T(4,128)} %reshape.49), calls=%async_computation | async-start | bytes 262144 | tf_op jit(solution)/shard_map/all_to_all | solution.py:69
  20.0 0.0 copy-done
  20.0 15.3 %scatter_custom_fusion.1 = bf16[2048,1024]{1,0:T(8,128)(2,1)} fusion(s32[1024]{0:T(1024)S(1)} %get-tuple-element.7, bf16[1024,1024]{1,0:T(8,128)(2,1)S(1)} %copy-done, s32[1024]{0:T(1024)S(1)} %get-tuple-element.8, bf16[]{:T(256)} %constant.52.clone.1), kind=kCustom, calls=%fused_computation.6 | custom fusion | bytes 4194306 | tf_op jit(solution)/shard_map/scatter | solution.py:56
  35.3 0.0 all-to-all-done
  35.3 10.5 %all-to-all-start.2 = ((bf16[64,4,8,1024]{3,2,1,0:T(8,128)(2,1)}), bf16[64,4,8,1024]{3,2,1,0:T(8,128)(2,1)}, u32[]{:S(2)}, u32[]{:S(2)}) async-start(bf16[64,4,8,1024]{3,2,1,0:T(8,128)(2,1)} %bitcast.20), calls=%async_computation.2 | async-start | bytes 8388608 | tf_op jit(solution)/shard_map/all_to_all | solution.py:62
  45.8 0.1 fusion.17
  45.9 0.1 copy.33
  46.0 0.1 copy.34
  46.0 0.1 copy.35
  46.1 0.1 copy.36
  46.1 0.7 reshape.89
  46.9 93.7 %all-to-all-done.2 = bf16[64,4,8,1024]{3,2,1,0:T(8,128)(2,1)} async-done(((bf16[64,4,8,1024]{3,2,1,0:T(8,128)(2,1)}), bf16[64,4,8,1024]{3,2,1,0:T(8,128)(2,1)}, u32[]{:S(2)}, u32[]{:S(2)}) %all-to-all-start.2) | async-done | bytes 4194336 | tf_op jit(solution)/shard_map/all_to_all | solution.py:62
  140.5 4.5 %all-to-all-start.1 = ((s32[4,1,512]{2,1,0:T(1,128)}), s32[4,1,512]{2,1,0:T(1,128)S(1)}, u32[]{:S(2)}, u32[]{:S(2)}) async-start(s32[4,1,512]{2,1,0:T(1,128)} %reshape.89), calls=%async_computation.1 | async-start | bytes 16384 | tf_op jit(solution)/shard_map/all_to_all | solution.py:11
  145.0 4.8 %copy.38 = bf16[64,4,8,1024]{3,2,0,1:T(8,128)(2,1)} copy(bf16[64,4,8,1024]{3,2,1,0:T(8,128)(2,1)} %all-to-all-done.2) | data formatting | bytes 8388608 | tf_op jit(solution)/shard_map/all_to_all | solution.py:62
  149.8 0.6 all-to-all-done.1
  150.3 4.9 %all-to-all-start.3 = ((bf16[64,4,8,1024]{3,2,0,1:T(8,128)(2,1)}), bf16[64,4,8,1024]{3,2,0,1:T(8,128)(2,1)}, u32[]{:S(2)}, u32[]{:S(2)}) async-start(bf16[64,4,8,1024]{3,2,0,1:T(8,128)(2,1)} %copy.38), calls=%async_computation.3 | async-start | bytes 8388608 | tf_op jit(solution)/shard_map/all_to_all | solution.py:61
  155.2 0.5 broadcast.69
  155.7 0.7 reduce
  156.4 0.1 reshape.90
  156.5 0.1 copy.37
  156.6 0.2 eq.55
  156.7 0.1 convert_reduce_fusion.1
  156.9 0.1 broadcast_in_dim_reshape.4
  157.0 0.1 add.55
  157.1 47.7 %all-to-all-done.3 = bf16[64,4,8,1024]{3,2,0,1:T(8,128)(2,1)} async-done(((bf16[64,4,8,1024]{3,2,0,1:T(8,128)(2,1)}), bf16[64,4,8,1024]{3,2,0,1:T(8,128)(2,1)}, u32[]{:S(2)}, u32[]{:S(2)}) %all-to-all-start.3) | async-done | bytes 4194336 | tf_op jit(solution)/shard_map/all_to_all | solution.py:61
  204.7 2.6 %copy.39 = bf16[64,4,8,1024]{3,2,1,0:T(8,128)(2,1)S(1)} copy(bf16[64,4,8,1024]{3,2,0,1:T(8,128)(2,1)} %all-to-all-done.3) | data formatting | bytes 8388608 | tf_op jit(solution)/shard_map/all_to_all | solution.py:61
  207.4 1.5 fusion.4
  208.9 12.4 %all_gather.3 = f32[8,8,1025]{2,1,0:T(8,128)S(1)} all-gather(f32[2,8,1025]{2,1,0:T(8,128)S(1)} %pad_maximum_fusion), channel_id=1, replica_groups=mesh['grp'=4,'dev'=64] {'grp'}, dimensions={0}, use_global_device_ids=true | all-gather | bytes 328000 | tf_op jit(solution)/shard_map/all_gather | solution.py:20
  221.4 0.7 split.28
  222.1 0.1 copy.42
  222.2 0.6 convert_bitcast_fusion
  (6 shorter events, 0.0 us)
Async XLA Ops:
  0.6 19.3 %copy-start = (bf16[1024,1024]{1,0:T(8,128)(2,1)S(1)}, bf16[1024,1024]{1,0:T(8,128)(2,1)}, u32[]{:S(2)}) copy-start(bf16[1024,1024]{1,0:T(8,128)(2,1)} %param.5) | copy-start | bytes 6291460
  7.9 27.4 %all-to-all-start = ((s32[64,4,8]{2,1,0:T(4,128)}), s32[64,4,8]{2,1,0:T(4,128)S(1)}, u32[]{:S(2)}, u32[]{:S(2)}) async-start(s32[64,4,8]{2,1,0:T(4,128)} %reshape.49), calls=%async_computation | async-start | bytes 262144 | tf_op jit(solution)/shard_map/all_to_all | solution.py:69
  35.3 105.3 %all-to-all-start.2 = ((bf16[64,4,8,1024]{3,2,1,0:T(8,128)(2,1)}), bf16[64,4,8,1024]{3,2,1,0:T(8,128)(2,1)}, u32[]{:S(2)}, u32[]{:S(2)}) async-start(bf16[64,4,8,1024]{3,2,1,0:T(8,128)(2,1)} %bitcast.20), calls=%async_computation.2 | async-start | bytes 8388608 | tf_op jit(solution)/shard_map/all_to_all | solution.py:62
  140.5 9.8 %all-to-all-start.1 = ((s32[4,1,512]{2,1,0:T(1,128)}), s32[4,1,512]{2,1,0:T(1,128)S(1)}, u32[]{:S(2)}, u32[]{:S(2)}) async-start(s32[4,1,512]{2,1,0:T(1,128)} %reshape.89), calls=%async_computation.1 | async-start | bytes 16384 | tf_op jit(solution)/shard_map/all_to_all | solution.py:11
  150.3 54.4 %all-to-all-start.3 = ((bf16[64,4,8,1024]{3,2,0,1:T(8,128)(2,1)}), bf16[64,4,8,1024]{3,2,0,1:T(8,128)(2,1)}, u32[]{:S(2)}, u32[]{:S(2)}) async-start(bf16[64,4,8,1024]{3,2,0,1:T(8,128)(2,1)} %copy.38), calls=%async_computation.3 | async-start | bytes 8388608 | tf_op jit(solution)/shard_map/all_to_all | solution.py:61
